TPU v7x, 32 devices: a 4x4x1 block of a 4x4x8 slice. The times are simulated.
32 devices in a mesh: data: 1 (over z), stage: 4 (over y), tp: 8 (over x, core).
Axes of the slice: x: 4, y: 4, z: 1, core: 2. Of those that a mesh axis runs over, the one named last changes fastest.
The devices are a block of a 4x4x8 slice.
Arguments:
- x_in: bfloat16 [32, 64, 4096], P('data')
- ln_gain: bfloat16 [4, 4096], P('stage')
- w_up: bfloat16 [4, 4096, 14336], P('stage', None, 'tp')
- w_down: bfloat16 [4, 14336, 4096], P('stage', 'tp')
Outputs:
- output: bfloat16 [4, 32, 64, 4096], P('stage', 'data')
All inputs are finite; a program needn't handle non-finite values.
Results may differ from a plain program's by a relative error of at most 0.0161352.
Values are sent between devices in bfloat16 or wider.
A program may use at most 768 MiB of HBM per device.

v0:
```python
import jax
import jax.numpy as jnp
from jax import lax
from jax.sharding import PartitionSpec as P

EPS = 1e-5


def layer_norm(y_prev, gain_wide):
    y_wide = y_prev.astype(jnp.float32)
    centered = y_wide - jnp.mean(y_wide, axis=-1, keepdims=True)
    variance = jnp.mean(centered * centered, axis=-1, keepdims=True)
    return (centered * lax.rsqrt(variance + EPS) * gain_wide).astype(jnp.bfloat16)


def local_block(y_prev, gain_wide, up_mat, down_mat):
    normed = layer_norm(y_prev, gain_wide)
    hidden = jax.nn.gelu(jnp.dot(normed, up_mat, preferred_element_type=jnp.float32), approximate=True).astype(jnp.bfloat16)
    partial_out = jnp.dot(hidden, down_mat, preferred_element_type=jnp.float32).astype(jnp.bfloat16)
    summed = lax.psum(partial_out, "tp")
    return (y_prev.astype(jnp.float32) + summed.astype(jnp.float32)).astype(jnp.bfloat16)


def solution(mesh):
    n_stage = mesh.shape["stage"]
    n_tp = mesh.shape["tp"]
    forward_perm = [(idx, idx + 1) for idx in range(n_stage - 1)]

    def per_device(x_local, gain_local, up_local, down_local):
        micro, tokens, width = x_local.shape
        piece_rows = tokens // n_tp
        stage_id = lax.axis_index("stage")
        tp_rank = lax.axis_index("tp")
        gain_wide = gain_local[0].astype(jnp.float32)
        up_mat = up_local[0]
        down_mat = down_local[0]

        def tick(step, carry):
            received, out_buf = carry
            gathered = lax.all_gather(received, "tp", axis=0, tiled=True)
            fresh = lax.dynamic_index_in_dim(x_local, jnp.minimum(step, micro - 1), 0, keepdims=False)
            block_in = jnp.where(stage_id == 0, fresh, gathered)
            block_out = local_block(block_in, gain_wide, up_mat, down_mat)
            micro_idx = step - stage_id
            slot = jnp.clip(micro_idx, 0, micro - 1)
            previous = lax.dynamic_index_in_dim(out_buf, slot, 0, keepdims=False)
            valid = (micro_idx >= 0) & (micro_idx < micro)
            out_buf = lax.dynamic_update_index_in_dim(out_buf, jnp.where(valid, block_out, previous), slot, 0)
            my_piece = lax.dynamic_slice_in_dim(block_out, tp_rank * piece_rows, piece_rows, 0)
            received = lax.ppermute(my_piece, "stage", forward_perm)
            return received, out_buf

        carry_init = (jnp.zeros((piece_rows, width), jnp.bfloat16), jnp.zeros_like(x_local))
        out_buf = lax.fori_loop(0, micro + n_stage - 1, tick, carry_init)[1]
        return out_buf[None]

    return jax.shard_map(per_device, mesh=mesh, in_specs=(P("data"), P("stage"), P("stage", None, "tp"), P("stage", "tp", None)), out_specs=P("stage", "data"), check_vma=False)
```

profile of v0, /device:TPU:121, one launch (start us, length us, event | category | flops | bytes accessed | tf_op | source)
XLA Modules:
  0.0 3665.0 jit_solution(5481439650718623964)
XLA Ops:
  13.4 3645.0 %while.17 = (s32[]{:T(128)}, bf16[8,4096]{1,0:T(8,128)(2,1)S(1)}, bf16[32,64,4096]{2,1,0:T(8,128)(2,1)}, pred[]{:T(512)}, bf16[32,64,4096]{2,1,0:T(8,128)(2,1)},...) while((s32[]{:T(128)}, bf16[8,4096]{1,0:T(8,128)(2,1)S(1)}, ...), condition=%wide.region_4.5_spmd, body=%wide.region_0.4_spmd.sunk | while | flops 1885061248 | bytes 40323660 | solution.py:54
  362.0 58.8 %all-reduce.2.cloned.1.call-done = bf16[64,4096]{1,0:T(8,128)(2,1)} async-done(((bf16[64,4096]{1,0:T(8,128)(2,1)}), bf16[64,4096]{1,0:T(8,128)(2,1)}) %all-reduce.2.cloned.1.call-update) | async-done | bytes 524304 | tf_op jit(solution)/shard_map/while/body/eval_jaxpr/psum | solution.py:20
  466.2 58.8 %all-reduce.2.cloned.1.call-done = bf16[64,4096]{1,0:T(8,128)(2,1)} async-done(((bf16[64,4096]{1,0:T(8,128)(2,1)}), bf16[64,4096]{1,0:T(8,128)(2,1)}) %all-reduce.2.cloned.1.call-update) | async-done | bytes 524304 | tf_op jit(solution)/shard_map/while/body/eval_jaxpr/psum | solution.py:20
  570.4 58.8 %all-reduce.2.cloned.1.call-done = bf16[64,4096]{1,0:T(8,128)(2,1)} async-done(((bf16[64,4096]{1,0:T(8,128)(2,1)}), bf16[64,4096]{1,0:T(8,128)(2,1)}) %all-reduce.2.cloned.1.call-update) | async-done | bytes 524304 | tf_op jit(solution)/shard_map/while/body/eval_jaxpr/psum | solution.py:20
  674.7 58.8 %all-reduce.2.cloned.1.call-done = bf16[64,4096]{1,0:T(8,128)(2,1)} async-done(((bf16[64,4096]{1,0:T(8,128)(2,1)}), bf16[64,4096]{1,0:T(8,128)(2,1)}) %all-reduce.2.cloned.1.call-update) | async-done | bytes 524304 | tf_op jit(solution)/shard_map/while/body/eval_jaxpr/psum | solution.py:20
  778.9 58.8 %all-reduce.2.cloned.1.call-done = bf16[64,4096]{1,0:T(8,128)(2,1)} async-done(((bf16[64,4096]{1,0:T(8,128)(2,1)}), bf16[64,4096]{1,0:T(8,128)(2,1)}) %all-reduce.2.cloned.1.call-update) | async-done | bytes 524304 | tf_op jit(solution)/shard_map/while/body/eval_jaxpr/psum | solution.py:20
  883.1 58.8 %all-reduce.2.cloned.1.call-done = bf16[64,4096]{1,0:T(8,128)(2,1)} async-done(((bf16[64,4096]{1,0:T(8,128)(2,1)}), bf16[64,4096]{1,0:T(8,128)(2,1)}) %all-reduce.2.cloned.1.call-update) | async-done | bytes 524304 | tf_op jit(solution)/shard_map/while/body/eval_jaxpr/psum | solution.py:20
  987.3 58.8 %all-reduce.2.cloned.1.call-done = bf16[64,4096]{1,0:T(8,128)(2,1)} async-done(((bf16[64,4096]{1,0:T(8,128)(2,1)}), bf16[64,4096]{1,0:T(8,128)(2,1)}) %all-reduce.2.cloned.1.call-update) | async-done | bytes 524304 | tf_op jit(solution)/shard_map/while/body/eval_jaxpr/psum | solution.py:20
  1091.5 58.8 %all-reduce.2.cloned.1.call-done = bf16[64,4096]{1,0:T(8,128)(2,1)} async-done(((bf16[64,4096]{1,0:T(8,128)(2,1)}), bf16[64,4096]{1,0:T(8,128)(2,1)}) %all-reduce.2.cloned.1.call-update) | async-done | bytes 524304 | tf_op jit(solution)/shard_map/while/body/eval_jaxpr/psum | solution.py:20
  1195.7 58.8 %all-reduce.2.cloned.1.call-done = bf16[64,4096]{1,0:T(8,128)(2,1)} async-done(((bf16[64,4096]{1,0:T(8,128)(2,1)}), bf16[64,4096]{1,0:T(8,128)(2,1)}) %all-reduce.2.cloned.1.call-update) | async-done | bytes 524304 | tf_op jit(solution)/shard_map/while/body/eval_jaxpr/psum | solution.py:20
  1299.9 58.8 %all-reduce.2.cloned.1.call-done = bf16[64,4096]{1,0:T(8,128)(2,1)} async-done(((bf16[64,4096]{1,0:T(8,128)(2,1)}), bf16[64,4096]{1,0:T(8,128)(2,1)}) %all-reduce.2.cloned.1.call-update) | async-done | bytes 524304 | tf_op jit(solution)/shard_map/while/body/eval_jaxpr/psum | solution.py:20
  1404.1 58.8 %all-reduce.2.cloned.1.call-done = bf16[64,4096]{1,0:T(8,128)(2,1)} async-done(((bf16[64,4096]{1,0:T(8,128)(2,1)}), bf16[64,4096]{1,0:T(8,128)(2,1)}) %all-reduce.2.cloned.1.call-update) | async-done | bytes 524304 | tf_op jit(solution)/shard_map/while/body/eval_jaxpr/psum | solution.py:20
  1508.3 58.8 %all-reduce.2.cloned.1.call-done = bf16[64,4096]{1,0:T(8,128)(2,1)} async-done(((bf16[64,4096]{1,0:T(8,128)(2,1)}), bf16[64,4096]{1,0:T(8,128)(2,1)}) %all-reduce.2.cloned.1.call-update) | async-done | bytes 524304 | tf_op jit(solution)/shard_map/while/body/eval_jaxpr/psum | solution.py:20
  1612.6 58.8 %all-reduce.2.cloned.1.call-done = bf16[64,4096]{1,0:T(8,128)(2,1)} async-done(((bf16[64,4096]{1,0:T(8,128)(2,1)}), bf16[64,4096]{1,0:T(8,128)(2,1)}) %all-reduce.2.cloned.1.call-update) | async-done | bytes 524304 | tf_op jit(solution)/shard_map/while/body/eval_jaxpr/psum | solution.py:20
  1716.8 58.8 %all-reduce.2.cloned.1.call-done = bf16[64,4096]{1,0:T(8,128)(2,1)} async-done(((bf16[64,4096]{1,0:T(8,128)(2,1)}), bf16[64,4096]{1,0:T(8,128)(2,1)}) %all-reduce.2.cloned.1.call-update) | async-done | bytes 524304 | tf_op jit(solution)/shard_map/while/body/eval_jaxpr/psum | solution.py:20
  1821.0 58.8 %all-reduce.2.cloned.1.call-done = bf16[64,4096]{1,0:T(8,128)(2,1)} async-done(((bf16[64,4096]{1,0:T(8,128)(2,1)}), bf16[64,4096]{1,0:T(8,128)(2,1)}) %all-reduce.2.cloned.1.call-update) | async-done | bytes 524304 | tf_op jit(solution)/shard_map/while/body/eval_jaxpr/psum | solution.py:20
  1925.2 58.8 %all-reduce.2.cloned.1.call-done = bf16[64,4096]{1,0:T(8,128)(2,1)} async-done(((bf16[64,4096]{1,0:T(8,128)(2,1)}), bf16[64,4096]{1,0:T(8,128)(2,1)}) %all-reduce.2.cloned.1.call-update) | async-done | bytes 524304 | tf_op jit(solution)/shard_map/while/body/eval_jaxpr/psum | solution.py:20
  2029.4 58.8 %all-reduce.2.cloned.1.call-done = bf16[64,4096]{1,0:T(8,128)(2,1)} async-done(((bf16[64,4096]{1,0:T(8,128)(2,1)}), bf16[64,4096]{1,0:T(8,128)(2,1)}) %all-reduce.2.cloned.1.call-update) | async-done | bytes 524304 | tf_op jit(solution)/shard_map/while/body/eval_jaxpr/psum | solution.py:20
  2133.6 58.8 %all-reduce.2.cloned.1.call-done = bf16[64,4096]{1,0:T(8,128)(2,1)} async-done(((bf16[64,4096]{1,0:T(8,128)(2,1)}), bf16[64,4096]{1,0:T(8,128)(2,1)}) %all-reduce.2.cloned.1.call-update) | async-done | bytes 524304 | tf_op jit(solution)/shard_map/while/body/eval_jaxpr/psum | solution.py:20
  2237.8 58.8 %all-reduce.2.cloned.1.call-done = bf16[64,4096]{1,0:T(8,128)(2,1)} async-done(((bf16[64,4096]{1,0:T(8,128)(2,1)}), bf16[64,4096]{1,0:T(8,128)(2,1)}) %all-reduce.2.cloned.1.call-update) | async-done | bytes 524304 | tf_op jit(solution)/shard_map/while/body/eval_jaxpr/psum | solution.py:20
  2342.0 58.8 %all-reduce.2.cloned.1.call-done = bf16[64,4096]{1,0:T(8,128)(2,1)} async-done(((bf16[64,4096]{1,0:T(8,128)(2,1)}), bf16[64,4096]{1,0:T(8,128)(2,1)}) %all-reduce.2.cloned.1.call-update) | async-done | bytes 524304 | tf_op jit(solution)/shard_map/while/body/eval_jaxpr/psum | solution.py:20
  2446.2 58.8 %all-reduce.2.cloned.1.call-done = bf16[64,4096]{1,0:T(8,128)(2,1)} async-done(((bf16[64,4096]{1,0:T(8,128)(2,1)}), bf16[64,4096]{1,0:T(8,128)(2,1)}) %all-reduce.2.cloned.1.call-update) | async-done | bytes 524304 | tf_op jit(solution)/shard_map/while/body/eval_jaxpr/psum | solution.py:20
  2550.4 58.8 %all-reduce.2.cloned.1.call-done = bf16[64,4096]{1,0:T(8,128)(2,1)} async-done(((bf16[64,4096]{1,0:T(8,128)(2,1)}), bf16[64,4096]{1,0:T(8,128)(2,1)}) %all-reduce.2.cloned.1.call-update) | async-done | bytes 524304 | tf_op jit(solution)/shard_map/while/body/eval_jaxpr/psum | solution.py:20
  2967.3 58.8 %all-reduce.2.cloned.1.call-done = bf16[64,4096]{1,0:T(8,128)(2,1)} async-done(((bf16[64,4096]{1,0:T(8,128)(2,1)}), bf16[64,4096]{1,0:T(8,128)(2,1)}) %all-reduce.2.cloned.1.call-update) | async-done | bytes 524304 | tf_op jit(solution)/shard_map/while/body/eval_jaxpr/psum | solution.py:20
  (470 shorter events, 2298.6 us)
Async XLA Ops:
  219.5 97.1 %all-reduce.2.cloned.1.call-start = ((), (), s32[]{:S(2)}) async-start(), calls=%async_computation | async-start | bytes 1048576 | tf_op jit(solution)/shard_map/while/body/eval_jaxpr/psum | solution.py:20
  323.7 97.1 %all-reduce.2.cloned.1.call-start = ((), (), s32[]{:S(2)}) async-start(), calls=%async_computation | async-start | bytes 1048576 | tf_op jit(solution)/shard_map/while/body/eval_jaxpr/psum | solution.py:20
  427.9 97.1 %all-reduce.2.cloned.1.call-start = ((), (), s32[]{:S(2)}) async-start(), calls=%async_computation | async-start | bytes 1048576 | tf_op jit(solution)/shard_map/while/body/eval_jaxpr/psum | solution.py:20
  532.1 97.1 %all-reduce.2.cloned.1.call-start = ((), (), s32[]{:S(2)}) async-start(), calls=%async_computation | async-start | bytes 1048576 | tf_op jit(solution)/shard_map/while/body/eval_jaxpr/psum | solution.py:20
  636.3 97.1 %all-reduce.2.cloned.1.call-start = ((), (), s32[]{:S(2)}) async-start(), calls=%async_computation | async-start | bytes 1048576 | tf_op jit(solution)/shard_map/while/body/eval_jaxpr/psum | solution.py:20
  740.5 97.1 %all-reduce.2.cloned.1.call-start = ((), (), s32[]{:S(2)}) async-start(), calls=%async_computation | async-start | bytes 1048576 | tf_op jit(solution)/shard_map/while/body/eval_jaxpr/psum | solution.py:20
  844.7 97.1 %all-reduce.2.cloned.1.call-start = ((), (), s32[]{:S(2)}) async-start(), calls=%async_computation | async-start | bytes 1048576 | tf_op jit(solution)/shard_map/while/body/eval_jaxpr/psum | solution.py:20
  948.9 97.1 %all-reduce.2.cloned.1.call-start = ((), (), s32[]{:S(2)}) async-start(), calls=%async_computation | async-start | bytes 1048576 | tf_op jit(solution)/shard_map/while/body/eval_jaxpr/psum | solution.py:20
  1053.1 97.1 %all-reduce.2.cloned.1.call-start = ((), (), s32[]{:S(2)}) async-start(), calls=%async_computation | async-start | bytes 1048576 | tf_op jit(solution)/shard_map/while/body/eval_jaxpr/psum | solution.py:20
  1157.4 97.1 %all-reduce.2.cloned.1.call-start = ((), (), s32[]{:S(2)}) async-start(), calls=%async_computation | async-start | bytes 1048576 | tf_op jit(solution)/shard_map/while/body/eval_jaxpr/psum | solution.py:20
  1261.6 97.1 %all-reduce.2.cloned.1.call-start = ((), (), s32[]{:S(2)}) async-start(), calls=%async_computation | async-start | bytes 1048576 | tf_op jit(solution)/shard_map/while/body/eval_jaxpr/psum | solution.py:20
  1365.8 97.1 %all-reduce.2.cloned.1.call-start = ((), (), s32[]{:S(2)}) async-start(), calls=%async_computation | async-start | bytes 1048576 | tf_op jit(solution)/shard_map/while/body/eval_jaxpr/psum | solution.py:20
  1470.0 97.1 %all-reduce.2.cloned.1.call-start = ((), (), s32[]{:S(2)}) async-start(), calls=%async_computation | async-start | bytes 1048576 | tf_op jit(solution)/shard_map/while/body/eval_jaxpr/psum | solution.py:20
  1574.2 97.1 %all-reduce.2.cloned.1.call-start = ((), (), s32[]{:S(2)}) async-start(), calls=%async_computation | async-start | bytes 1048576 | tf_op jit(solution)/shard_map/while/body/eval_jaxpr/psum | solution.py:20
  1678.4 97.1 %all-reduce.2.cloned.1.call-start = ((), (), s32[]{:S(2)}) async-start(), calls=%async_computation | async-start | bytes 1048576 | tf_op jit(solution)/shard_map/while/body/eval_jaxpr/psum | solution.py:20
  1782.6 97.1 %all-reduce.2.cloned.1.call-start = ((), (), s32[]{:S(2)}) async-start(), calls=%async_computation | async-start | bytes 1048576 | tf_op jit(solution)/shard_map/while/body/eval_jaxpr/psum | solution.py:20
  1886.8 97.1 %all-reduce.2.cloned.1.call-start = ((), (), s32[]{:S(2)}) async-start(), calls=%async_computation | async-start | bytes 1048576 | tf_op jit(solution)/shard_map/while/body/eval_jaxpr/psum | solution.py:20
  1991.0 97.1 %all-reduce.2.cloned.1.call-start = ((), (), s32[]{:S(2)}) async-start(), calls=%async_computation | async-start | bytes 1048576 | tf_op jit(solution)/shard_map/while/body/eval_jaxpr/psum | solution.py:20
  2095.3 97.1 %all-reduce.2.cloned.1.call-start = ((), (), s32[]{:S(2)}) async-start(), calls=%async_computation | async-start | bytes 1048576 | tf_op jit(solution)/shard_map/while/body/eval_jaxpr/psum | solution.py:20
  2199.5 97.1 %all-reduce.2.cloned.1.call-start = ((), (), s32[]{:S(2)}) async-start(), calls=%async_computation | async-start | bytes 1048576 | tf_op jit(solution)/shard_map/while/body/eval_jaxpr/psum | solution.py:20
  2303.7 97.1 %all-reduce.2.cloned.1.call-start = ((), (), s32[]{:S(2)}) async-start(), calls=%async_computation | async-start | bytes 1048576 | tf_op jit(solution)/shard_map/while/body/eval_jaxpr/psum | solution.py:20
  2407.9 97.1 %all-reduce.2.cloned.1.call-start = ((), (), s32[]{:S(2)}) async-start(), calls=%async_computation | async-start | bytes 1048576 | tf_op jit(solution)/shard_map/while/body/eval_jaxpr/psum | solution.py:20
  2512.1 97.1 %all-reduce.2.cloned.1.call-start = ((), (), s32[]{:S(2)}) async-start(), calls=%async_computation | async-start | bytes 1048576 | tf_op jit(solution)/shard_map/while/body/eval_jaxpr/psum | solution.py:20
  2616.3 97.1 %all-reduce.2.cloned.1.call-start = ((), (), s32[]{:S(2)}) async-start(), calls=%async_computation | async-start | bytes 1048576 | tf_op jit(solution)/shard_map/while/body/eval_jaxpr/psum | solution.py:20
  (46 other events, 1241.8 us)
Sparse Core Ops, SparseCore 0:
  361.1 59.6 all-reduce.1
  465.3 59.6 all-reduce.1
  569.5 59.6 all-reduce.1
  673.7 59.6 all-reduce.1
  777.9 59.6 all-reduce.1
  986.3 59.6 all-reduce.1
  1090.5 59.6 all-reduce.1
  1298.9 59.6 all-reduce.1
  1403.2 59.6 all-reduce.1
  1611.6 59.6 all-reduce.1
  1715.8 59.6 all-reduce.1
  1924.2 59.6 all-reduce.1
  2028.4 59.6 all-reduce.1
  2132.6 59.6 all-reduce.1
  2236.8 59.6 all-reduce.1
  2341.1 59.6 all-reduce.1
  2445.3 59.6 all-reduce.1
  2653.7 59.6 all-reduce.1
  2757.9 59.6 all-reduce.1
  2966.3 59.6 all-reduce.1
  3070.5 59.6 all-reduce.1
  3278.9 59.6 all-reduce.1
  3383.2 59.6 all-reduce.1
  3591.6 59.6 all-reduce.1
  (11 shorter events, 654.8 us)
where the time goes:
time: 3680 us; the launch traced here: 3660 us
  waiting for transfers between devices  2190 us (60%)
  blocking collectives  695 us (19%)
  matrix products  548 us (15%)
  other arithmetic  130 us (4%)
  starting transfers between devices  45.4 us (1%)
  local copies, waits for them, and re-layouts  44.1 us (1%)
    psum x35, waiting for transfers between devices, local_block(): summed = lax.psum(partial_out, 'tp')  2060 us
    all_gather x35, blocking collectives, tick(): gathered = lax.all_gather(received, 'tp', axis=0, tiled=True)  695 us
    dot_general x35, matrix products, local_block(): jnp.dot(hidden, down_mat, preferred_element_type=jnp.float32)  548 us
    ppermute x35, waiting for transfers between devices, tick(): received = lax.ppermute(my_piece, 'stage', forward_perm)  130 us
  transfers between devices with their start and end apart: 70, of which 70 were waited for; matrix products, arithmetic and copies ran while one was open for 1% of the time, Pallas kernels for 0%

commit v1 on v0

v1 whole, which is shorter than its diff:
```python
import functools

import jax
import jax.numpy as jnp
from jax import lax
from jax.experimental import pallas as pl
from jax.experimental.pallas import tpu as pltpu
from jax.sharding import PartitionSpec as P

EPS = 1e-5
MESH = pl.DeviceIdType.MESH
CORES = 2
MERGE = 2
SLOTS = 3
STAGING = 3
LAG_FIRST = 13
LAG_RELAY = 6
LN_ROWS = 64
F32, BF16 = jnp.float32, jnp.bfloat16


def mlp_kernel(
    n_stage, n_tp, x_hbm, gain_ref, up_hbm, down_hbm, y_hbm,
    up, down, acts, normed, hidden, part, pair, lead, ring1, direct, ring2, carry, shard,
    w_sem, x_sem, own_r, side_r, opp_r, mate_r, back_r, relay_r, out_r,
    pair_r, ring1_r, direct_r, ring2_r,
    side_s, mate_s, fwd_s, back_s, relay_s, pair_s, ring1_s, direct_s, ring2_s, next_s, out_s, keep_s,
):
    groups, blocks, rows, width = x_hbm.shape
    half = width // 2
    chips = n_tp // CORES
    stage = lax.axis_index("stage")
    rank = lax.axis_index("tp")
    chip, core = rank // CORES, lax.rem(rank, CORES)
    first = stage == 0

    def at_chip(step):
        return lax.rem(chip + step, chips)

    right_c, left_c, opp_c = at_chip(1), at_chip(chips - 1), at_chip(2)
    mate = {"tp": chip * CORES + (1 - core)}
    right = {"tp": right_c * CORES + core}
    left = {"tp": left_c * CORES + core}
    ahead = {"stage": lax.rem(stage + 1, n_stage)}
    behind = {"stage": lax.rem(stage + n_stage - 1, n_stage)}
    block_r, block_l, block_o = right_c * CORES + core, left_c * CORES + core, opp_c * CORES + core
    cols = (pl.ds(0, half), pl.ds(half, half))

    def remote(src, dst, send, recv, device):
        return pltpu.make_async_remote_copy(
            src_ref=src, dst_ref=dst, send_sem=send, recv_sem=recv, device_id=device, device_id_type=MESH
        )

    def when_group(g):
        return pl.when((g >= 0) & (g < groups))

    barrier = pltpu.get_barrier_semaphore()
    for peer in (mate, right, left, ahead, behind):
        pl.semaphore_signal(barrier, inc=1, device_id=peer, device_id_type=MESH)

    load_up = pltpu.make_async_copy(up_hbm.at[0], up, w_sem.at[0])
    load_down = pltpu.make_async_copy(down_hbm.at[0], down, w_sem.at[1])
    load_up.start()

    def load_x(g):
        return pltpu.make_async_copy(x_hbm.at[g], acts.at[groups + lax.rem(g, STAGING)], x_sem.at[lax.rem(g, STAGING)])

    @pl.when(first)
    def _():
        load_x(0).start()

    load_down.start()
    pl.semaphore_wait(barrier, 5)

    def in_slot(g):
        return jnp.where(first, groups + lax.rem(g, STAGING), g)

    def side_copy(g, way):
        return remote(acts.at[g, rank], acts.at[g, rank], side_s.at[lax.rem(g, 4), way], side_r.at[g, way], (right, left)[way])

    def fwd_copy(g, way):
        block = (block_l, block_r)[way]
        ref = acts.at[g, block, :, cols[way]]
        return remote(ref, ref, fwd_s.at[lax.rem(g, 4), way], opp_r.at[g, way], (right, left)[way])

    def mate_copy(g, which):
        block = (rank, block_l, block_r, block_o)[which]
        return remote(acts.at[g, block], acts.at[g, block], mate_s.at[lax.rem(g, 4), which], mate_r.at[g, which], mate)

    def back_copy(g, which):
        block = (block_l, block_r, block_o)[which]
        return remote(acts.at[g, block], y_hbm.at[g, block], back_s.at[lax.rem(g, 4), which], back_r.at[g, which], behind)

    def next_copy(g):
        slot = lax.rem(g, 2)
        return remote(shard.at[slot], acts.at[g, rank], next_s.at[slot], own_r.at[g], ahead)

    def gather_own(g):
        @when_group(g)
        def _():
            next_copy(g).wait_recv()
            side_copy(g, 0).start()
            side_copy(g, 1).start()

            @pl.when(jnp.logical_not(first))
            def _():
                mate_copy(g, 0).start()

    def gather_sides(g):
        @when_group(g)
        def _():
            side_copy(g, 0).wait_recv()
            side_copy(g, 1).wait_recv()
            fwd_copy(g, 0).start()
            fwd_copy(g, 1).start()

            @pl.when(jnp.logical_not(first))
            def _():
                mate_copy(g, 1).start()
                mate_copy(g, 2).start()

            back_copy(g, 0).start()
            back_copy(g, 1).start()

    def gather_opposite(g):
        @when_group(g)
        def _():
            fwd_copy(g, 0).wait_recv()
            fwd_copy(g, 1).wait_recv()

            @pl.when(jnp.logical_not(first))
            def _():
                mate_copy(g, 3).start()

            back_copy(g, 2).start()

    def gather_mate(g):
        @pl.when((g >= 0) & (g < groups) & jnp.logical_not(first))
        def _():
            for which in range(4):
                mate_copy(g, which).wait_recv()

    def gather_sent(g):
        @when_group(g)
        def _():
            for way in range(2):
                side_copy(g, way).wait_send()
                fwd_copy(g, way).wait_send()
            for which in range(3):
                back_copy(g, which).wait_send()

            @pl.when(jnp.logical_not(first))
            def _():
                for which in range(4):
                    mate_copy(g, which).wait_send()

    def pair_copy(g, h):
        slot, to = lax.rem(g, 2), lax.rem(g, SLOTS)
        return remote(
            part.at[slot, 1 - core, :, :, cols[h]], pair.at[to, :, :, cols[h]], pair_s.at[slot, h], pair_r.at[to, h], mate
        )

    def ring1_copy(g, h):
        slot, to = lax.rem(g, 2), lax.rem(g, SLOTS)
        return remote(lead.at[slot, h, 0], ring1.at[to, h], ring1_s.at[slot, h], ring1_r.at[to, h], (right, left)[h])

    def direct_copy(g, h):
        slot, to = lax.rem(g, 2), lax.rem(g, SLOTS)
        return remote(lead.at[slot, h, 1], direct.at[to, h], direct_s.at[slot, h], direct_r.at[to, h], (left, right)[h])

    def ring2_copy(g, h):
        slot, to = lax.rem(g, 2), lax.rem(g, SLOTS)
        return remote(carry.at[slot, h], ring2.at[to, h], ring2_s.at[slot, h], ring2_r.at[to, h], (right, left)[h])

    def pair_sum(g, c, h):
        return part[lax.rem(g, 2), core, c, :, cols[h]].astype(F32) + pair[lax.rem(g, SLOTS), c, :, cols[h]].astype(F32)

    def reduce_pair(g, h):
        @when_group(g)
        def _():
            slot = lax.rem(g, 2)
            pair_copy(g, h).wait_recv()
            lead[slot, h, 0] = pair_sum(g, opp_c, h).astype(BF16)
            lead[slot, h, 1] = pair_sum(g, (left_c, right_c)[h], h).astype(BF16)
            ring1_copy(g, h).start()
            direct_copy(g, h).start()

    def reduce_ring(g):
        @when_group(g)
        def _():
            slot = lax.rem(g, 2)
            for h in range(2):
                ring1_copy(g, h).wait_recv()
                total = pair_sum(g, (right_c, left_c)[h], h) + ring1[lax.rem(g, SLOTS), h].astype(F32)
                carry[slot, h] = total.astype(BF16)
                ring2_copy(g, h).start()

    def keep_copy(g):
        slot = lax.rem(g, 2)
        return pltpu.make_async_copy(shard.at[slot], y_hbm.at[g, rank], keep_s.at[slot])

    def out_copy(g):
        slot = lax.rem(g, 2)
        return remote(shard.at[slot], y_hbm.at[g, rank], out_s.at[slot], out_r.at[g], mate)

    def reduce_last(g):
        @when_group(g)
        def _():
            slot = lax.rem(g, 2)
            for h in range(2):
                direct_copy(g, h).wait_recv()
                ring2_copy(g, h).wait_recv()
            src = in_slot(g)
            for h in range(2):
                total = pair_sum(g, chip, h) + ring2[lax.rem(g, SLOTS), h].astype(F32) + direct[lax.rem(g, SLOTS), h].astype(F32)
                shard[slot, :, cols[h]] = (acts[src, rank, :, cols[h]].astype(F32) + total).astype(BF16)
            next_copy(g).start()
            keep_copy(g).start()
            out_copy(g).start()

    def reduce_sent(g):
        @when_group(g)
        def _():
            for h in range(2):
                pair_copy(g, h).wait_send()
                ring1_copy(g, h).wait_send()
                direct_copy(g, h).wait_send()

    def shard_sent(g):
        @when_group(g)
        def _():
            for h in range(2):
                ring2_copy(g, h).wait_send()
            next_copy(g).wait_send()
            keep_copy(g).wait()
            out_copy(g).wait_send()

    def relay_copy(g, which):
        block = (block_l, block_r, block_o)[which]
        ref = y_hbm.at[g, block]
        return remote(ref, ref, relay_s.at[lax.rem(g, 4), which], relay_r.at[g, which], mate)

    def relay(g):
        @when_group(g)
        def _():
            for which in range(3):
                back_copy(g, which).wait_recv()
                relay_copy(g, which).start()

    def relay_done(g):
        @when_group(g)
        def _():
            for which in range(3):
                relay_copy(g, which).wait()
            out_copy(g).wait_recv()

    def layer_norm(g):
        src = in_slot(g)
        gain = gain_ref[...].astype(F32)
        per = LN_ROWS // rows
        for piece in range(blocks // per):
            y = acts[src, pl.ds(piece * per, per)].reshape(LN_ROWS, width).astype(F32)
            centered = y - jnp.mean(y, axis=-1, keepdims=True)
            variance = jnp.mean(centered * centered, axis=-1, keepdims=True)
            normed[pl.ds(piece * LN_ROWS, LN_ROWS), :] = (centered * lax.rsqrt(variance + EPS) * gain).astype(BF16)

    def matmul_up():
        total = jnp.dot(normed[...], up[...], preferred_element_type=F32)
        hidden[...] = jax.nn.gelu(total, approximate=True).astype(BF16)

    def matmul_down(g, h):
        slot = lax.rem(g, 2)
        total = jnp.dot(hidden[...], down[:, cols[h]], preferred_element_type=F32).astype(BF16)
        for block in range(blocks):
            part[slot, block % CORES, block // CORES, :, cols[h]] = total[block * rows:(block + 1) * rows]
        pair_copy(g, h).start()

    gather_lag = jnp.where(first, -LAG_FIRST, 2)

    def step(i):
        ag = i + gather_lag
        reduce_sent(i - 2)
        shard_sent(i - 3)
        gather_sent(ag - 4)
        relay(i - LAG_RELAY)
        relay_done(i - LAG_RELAY - 2)
        gather_mate(ag - 2)

        @when_group(i)
        def _():
            @pl.when(first)
            def _():
                load_x(i).wait()

                @pl.when(i + 1 < groups)
                def _():
                    load_x(i + 1).start()

            layer_norm(i)

        reduce_pair(i - 1, 1)

        @when_group(i)
        def _():
            @pl.when(i == 0)
            def _():
                load_up.wait()

            matmul_up()

        reduce_ring(i - 1)
        gather_sides(ag - 1)

        @when_group(i)
        def _():
            @pl.when(i == 0)
            def _():
                load_down.wait()

            matmul_down(i, 0)
            matmul_down(i, 1)

        reduce_pair(i, 0)
        reduce_last(i - 1)
        gather_opposite(ag - 1)
        gather_own(ag)

    @pl.loop(-2, groups + LAG_FIRST + 5)
    def _(i):
        step(i)


def solution(mesh):
    n_stage = mesh.shape["stage"]
    n_tp = mesh.shape["tp"]

    def per_device(x_local, gain_local, up_local, down_local):
        micro, tokens, width = x_local.shape
        inner = up_local.shape[2]
        groups, size = micro // MERGE, MERGE * tokens
        rows = size // n_tp
        chips = n_tp // CORES
        half = width // 2
        x_blocks = x_local.reshape(groups, n_tp, rows, width)
        dma = pltpu.SemaphoreType.DMA
        out = pl.pallas_call(
            functools.partial(mlp_kernel, n_stage, n_tp),
            out_shape=jax.ShapeDtypeStruct(x_blocks.shape, BF16),
            in_specs=[
                pl.BlockSpec(memory_space=pl.ANY),
                pl.BlockSpec(memory_space=pltpu.VMEM),
                pl.BlockSpec(memory_space=pl.ANY),
                pl.BlockSpec(memory_space=pl.ANY),
            ],
            out_specs=pl.BlockSpec(memory_space=pl.ANY),
            scratch_shapes=[
                pltpu.VMEM((width, inner), BF16),
                pltpu.VMEM((inner, width), BF16),
                pltpu.VMEM((groups + STAGING, n_tp, rows, width), BF16),
                pltpu.VMEM((size, width), BF16),
                pltpu.VMEM((size, inner), BF16),
                pltpu.VMEM((2, CORES, chips, rows, width), BF16),
                pltpu.VMEM((SLOTS, chips, rows, width), BF16),
                pltpu.VMEM((2, 2, 2, rows, half), BF16),
                pltpu.VMEM((SLOTS, 2, rows, half), BF16),
                pltpu.VMEM((SLOTS, 2, rows, half), BF16),
                pltpu.VMEM((SLOTS, 2, rows, half), BF16),
                pltpu.VMEM((2, 2, rows, half), BF16),
                pltpu.VMEM((2, rows, width), BF16),
                dma((2,)), dma((STAGING,)),
                dma((groups,)), dma((groups, 2)), dma((groups, 2)), dma((groups, 4)),
                dma((groups, 3)), dma((groups, 3)), dma((groups,)),
                dma((SLOTS, 2)), dma((SLOTS, 2)), dma((SLOTS, 2)), dma((SLOTS, 2)),
                dma((4, 2)), dma((4, 4)), dma((4, 2)), dma((4, 3)), dma((4, 3)),
                dma((2, 2)), dma((2, 2)), dma((2, 2)), dma((2, 2)), dma((2,)), dma((2,)), dma((2,)),
            ],
            compiler_params=pltpu.CompilerParams(
                collective_id=0, has_side_effects=True, vmem_limit_bytes=66_000_000
            ),
            name="mlp_pipeline",
        )(x_blocks, gain_local, up_local, down_local)
        return out.reshape(1, micro, tokens, width)

    return jax.shard_map(per_device, mesh=mesh, in_specs=(P("data"), P("stage"), P("stage", None, "tp"), P("stage", "tp", None)), out_specs=P("stage", "data"), check_vma=False)
```

time: 3680 us -> 317 us (0.09)
  waiting for transfers between devices: 2190 us -> 0 us
  blocking collectives: 695 us -> 0 us
  matrix products: 548 us -> 0 us
  Pallas kernels: 0 us -> 302 us
  other arithmetic: 130 us -> 0 us
  starting transfers between devices: 45.4 us -> 0 us
    psum x35 -> x0, waiting for transfers between devices: 2060 us -> none  [local_block(): summed = lax.psum(partial_out, 'tp')]
    all_gather x35 -> x0, blocking collectives: 695 us -> none  [tick(): gathered = lax.all_gather(received, 'tp', axis=0, tiled=True)]
    dot_general x35 -> x0, matrix products: 548 us -> none  [local_block(): jnp.dot(hidden, down_mat, preferred_element_type=jnp.float32)]
    pallas_call x0 -> x1, Pallas kernels: none -> 302 us  [per_device(): pl.pallas_call(functools.partial(mlp_kernel, n_stage, n_tp), out_shape=ja...]
    ppermute x35 -> x0, waiting for transfers between devices: 130 us -> none  [tick(): received = lax.ppermute(my_piece, 'stage', forward_perm)]
    dynamic_update_slice x35 -> x0, other arithmetic: 72.3 us -> none  [tick(): lax.dynamic_update_index_in_dim(out_buf, jnp.where(valid, block_out, prev...]
    reduce_sum x70 -> x0, other arithmetic: 56.4 us -> none  [the longest x35 45.4 us: layer_norm(): centered = y_wide - jnp.mean(y_wide, axis=-1, keepdims=True)]
    ppermute x35 -> x0, starting transfers between devices: 45.4 us -> none  [tick(): received = lax.ppermute(my_piece, 'stage', forward_perm)]
  transfers between devices with their start and end apart: 70 -> 0, of which waited for: 70 -> 0; matrix products, arithmetic and copies ran while one was open for 1% -> 0% of each run, Pallas kernels for 0% -> 0%
where the time goes in v1:
time: 317 us; the launch traced here: 316 us
  Pallas kernels  302 us (95%)
  local copies, waits for them, and re-layouts  14.1 us (4%)
    pallas_call x1, Pallas kernels, per_device(): pl.pallas_call(functools.partial(mlp_kernel, n_stage, n_tp), out_shape=ja...  302 us
    unnamed x1, local copies, waits for them, and re-layouts  14.1 us

profile of v1, /device:TPU:121, one launch (start us, length us, event | category | flops | bytes accessed | tf_op | source)
XLA Modules:
  0.0 316.3 jit_solution(5553671624263634176)
XLA Ops:
  0.0 302.2 %mlp_pipeline.1 = bf16[16,8,16,4096]{3,2,1,0:T(8,128)(2,1)} custom-call(bf16[16,8,16,4096]{3,2,1,0:T(8,128)(2,1)} %bitcast.3, bf16[1,4096]{1,0:T(2,128)(2,1)} %gain_ref.1, bf16[1,4096,1792]{2,1,0:T(8,128)(2,1)} %up_hbm.1, bf16[1,1792,4096]{2,1,0:T(8,128)(2,1)} %down_hbm.1), custom_call_target="tpu_custom_call" | custom-call | tf_op jit(solution)/shard_map/mlp_pipeline/pallas_call | solution.py:346
  302.2 14.1 %copy.6 = bf16[1,32,64,4096]{3,2,1,0:T(8,128)(2,1)} copy(bf16[1,32,64,4096]{3,2,1,0:T(8,128)(2,1)} %bitcast.2) | data formatting | bytes 33554432

commit v2 on v1

--- a/solution.py
+++ b/solution.py
@@ -14,8 +14,11 @@
 SLOTS = 3
 STAGING = 3
 LAG_FIRST = 13
+TAIL = 2
 LAG_RELAY = 6
 LN_ROWS = 64
+UP_PIECES = 1
+ORDER = ("mate", "norm", "up0", "ring0", "ring1", "down0", "sides", "down1", "last", "pair0", "pair1", "own", "opp")
 F32, BF16 = jnp.float32, jnp.bfloat16
 
 
@@ -25,6 +28,7 @@
     w_sem, x_sem, own_r, side_r, opp_r, mate_r, back_r, relay_r, out_r,
     pair_r, ring1_r, direct_r, ring2_r,
     side_s, mate_s, fwd_s, back_s, relay_s, pair_s, ring1_s, direct_s, ring2_s, next_s, out_s, keep_s,
+    tail_r, tail_s, tail_fwd_s, tail_keep_s, tail_mate_s,
 ):
     groups, blocks, rows, width = x_hbm.shape
     half = width // 2
@@ -33,6 +37,8 @@
     rank = lax.axis_index("tp")
     chip, core = rank // CORES, lax.rem(rank, CORES)
     first = stage == 0
+    final = stage == n_stage - 1
+    gathers = jnp.where(first, groups - TAIL, groups)
 
     def at_chip(step):
         return lax.rem(chip + step, chips)
@@ -54,6 +60,15 @@
     def when_group(g):
         return pl.when((g >= 0) & (g < groups))
 
+    def when_gathered(g):
+        return pl.when((g >= 0) & (g < gathers))
+
+    def is_tail(g):
+        return final & (g >= groups - TAIL)
+
+    def when_tail(g):
+        return pl.when(final & (g >= groups - TAIL) & (g < groups))
+
     barrier = pltpu.get_barrier_semaphore()
     for peer in (mate, right, left, ahead, behind):
         pl.semaphore_signal(barrier, inc=1, device_id=peer, device_id_type=MESH)
@@ -96,7 +111,7 @@
         return remote(shard.at[slot], acts.at[g, rank], next_s.at[slot], own_r.at[g], ahead)
 
     def gather_own(g):
-        @when_group(g)
+        @when_gathered(g)
         def _():
             next_copy(g).wait_recv()
             side_copy(g, 0).start()
@@ -107,7 +122,7 @@
                 mate_copy(g, 0).start()
 
     def gather_sides(g):
-        @when_group(g)
+        @when_gathered(g)
         def _():
             side_copy(g, 0).wait_recv()
             side_copy(g, 1).wait_recv()
@@ -123,7 +138,7 @@
             back_copy(g, 1).start()
 
     def gather_opposite(g):
-        @when_group(g)
+        @when_gathered(g)
         def _():
             fwd_copy(g, 0).wait_recv()
             fwd_copy(g, 1).wait_recv()
@@ -141,7 +156,7 @@
                 mate_copy(g, which).wait_recv()
 
     def gather_sent(g):
-        @when_group(g)
+        @when_gathered(g)
         def _():
             for way in range(2):
                 side_copy(g, way).wait_send()
@@ -185,15 +200,66 @@
             ring1_copy(g, h).start()
             direct_copy(g, h).start()
 
-    def reduce_ring(g):
+    def reduce_ring(g, h):
         @when_group(g)
         def _():
             slot = lax.rem(g, 2)
-            for h in range(2):
-                ring1_copy(g, h).wait_recv()
-                total = pair_sum(g, (right_c, left_c)[h], h) + ring1[lax.rem(g, SLOTS), h].astype(F32)
-                carry[slot, h] = total.astype(BF16)
-                ring2_copy(g, h).start()
+            ring1_copy(g, h).wait_recv()
+            total = pair_sum(g, (right_c, left_c)[h], h) + ring1[lax.rem(g, SLOTS), h].astype(F32)
+            carry[slot, h] = total.astype(BF16)
+            ring2_copy(g, h).start()
+
+    def tail_side_copy(g, way):
+        index = g - (groups - TAIL)
+        return remote(
+            shard.at[lax.rem(g, 2)], acts.at[g + TAIL, rank], tail_s.at[index, way], tail_r.at[index, way], (right, left)[way]
+        )
+
+    def tail_fwd_copy(g, way):
+        index = g - (groups - TAIL)
+        ref = acts.at[g + TAIL, (block_l, block_r)[way], :, cols[way]]
+        return remote(ref, ref, tail_fwd_s.at[index, way], tail_r.at[index, 2 + way], (right, left)[way])
+
+    def tail_keep_copy(g, which):
+        index, block = g - (groups - TAIL), (block_l, block_r, block_o)[which]
+        return pltpu.make_async_copy(acts.at[g + TAIL, block], y_hbm.at[g, block], tail_keep_s.at[index, which])
+
+    def tail_mate_copy(g, which):
+        index, block = g - (groups - TAIL), (block_l, block_r, block_o)[which]
+        return remote(acts.at[g + TAIL, block], y_hbm.at[g, block], tail_mate_s.at[index, which], relay_r.at[g, which], mate)
+
+    def tail_own(g):
+        @when_tail(g)
+        def _():
+            tail_side_copy(g, 0).start()
+            tail_side_copy(g, 1).start()
+
+    def tail_sides(g):
+        @when_tail(g)
+        def _():
+            for way in range(2):
+                tail_side_copy(g, way).wait_recv()
+                tail_fwd_copy(g, way).start()
+            for which in range(2):
+                tail_mate_copy(g, which).start()
+                tail_keep_copy(g, which).start()
+
+    def tail_opposite(g):
+        @when_tail(g)
+        def _():
+            for way in range(2):
+                tail_fwd_copy(g, way).wait_recv()
+            tail_mate_copy(g, 2).start()
+            tail_keep_copy(g, 2).start()
+
+    def tail_done(g):
+        @when_tail(g)
+        def _():
+            for way in range(2):
+                tail_fwd_copy(g, way).wait_send()
+            for which in range(3):
+                tail_mate_copy(g, which).wait_send()
+                tail_keep_copy(g, which).wait()
 
     def keep_copy(g):
         slot = lax.rem(g, 2)
@@ -214,7 +280,10 @@
             for h in range(2):
                 total = pair_sum(g, chip, h) + ring2[lax.rem(g, SLOTS), h].astype(F32) + direct[lax.rem(g, SLOTS), h].astype(F32)
                 shard[slot, :, cols[h]] = (acts[src, rank, :, cols[h]].astype(F32) + total).astype(BF16)
-            next_copy(g).start()
+            @pl.when(jnp.logical_not(is_tail(g)))
+            def _():
+                next_copy(g).start()
+
             keep_copy(g).start()
             out_copy(g).start()
 
@@ -231,7 +300,16 @@
         def _():
             for h in range(2):
                 ring2_copy(g, h).wait_send()
-            next_copy(g).wait_send()
+
+            @pl.when(jnp.logical_not(is_tail(g)))
+            def _():
+                next_copy(g).wait_send()
+
+            @pl.when(is_tail(g))
+            def _():
+                tail_side_copy(g, 0).wait_send()
+                tail_side_copy(g, 1).wait_send()
+
             keep_copy(g).wait()
             out_copy(g).wait_send()
 
@@ -241,7 +319,7 @@
         return remote(ref, ref, relay_s.at[lax.rem(g, 4), which], relay_r.at[g, which], mate)
 
     def relay(g):
-        @when_group(g)
+        @pl.when((g >= 0) & (g < groups) & jnp.logical_not(is_tail(g)))
         def _():
             for which in range(3):
                 back_copy(g, which).wait_recv()
@@ -251,7 +329,12 @@
         @when_group(g)
         def _():
             for which in range(3):
-                relay_copy(g, which).wait()
+                relay_copy(g, which).wait_recv()
+
+                @pl.when(jnp.logical_not(is_tail(g)))
+                def _():
+                    relay_copy(g, which).wait_send()
+
             out_copy(g).wait_recv()
 
     def layer_norm(g):
@@ -264,9 +347,10 @@
             variance = jnp.mean(centered * centered, axis=-1, keepdims=True)
             normed[pl.ds(piece * LN_ROWS, LN_ROWS), :] = (centered * lax.rsqrt(variance + EPS) * gain).astype(BF16)
 
-    def matmul_up():
-        total = jnp.dot(normed[...], up[...], preferred_element_type=F32)
-        hidden[...] = jax.nn.gelu(total, approximate=True).astype(BF16)
+    def matmul_up(piece):
+        part_cols = pl.ds(piece * (hidden.shape[1] // UP_PIECES), hidden.shape[1] // UP_PIECES)
+        total = jnp.dot(normed[...], up[:, part_cols], preferred_element_type=F32)
+        hidden[:, part_cols] = jax.nn.gelu(total, approximate=True).astype(BF16)
 
     def matmul_down(g, h):
         slot = lax.rem(g, 2)
@@ -276,6 +360,39 @@
         pair_copy(g, h).start()
 
     gather_lag = jnp.where(first, -LAG_FIRST, 2)
+
+    def compute_norm(i):
+        @when_group(i)
+        def _():
+            @pl.when(first)
+            def _():
+                load_x(i).wait()
+
+                @pl.when(i + 1 < groups)
+                def _():
+                    load_x(i + 1).start()
+
+            layer_norm(i)
+
+    def compute_up(i, piece):
+        @when_group(i)
+        def _():
+            @pl.when(i == 0)
+            def _():
+                if piece == 0:
+                    load_up.wait()
+
+            matmul_up(piece)
+
+    def compute_down(i, h):
+        @when_group(i)
+        def _():
+            @pl.when(i == 0)
+            def _():
+                if h == 0:
+                    load_down.wait()
+
+            matmul_down(i, h)
 
     def step(i):
         ag = i + gather_lag
@@ -284,50 +401,43 @@
         gather_sent(ag - 4)
         relay(i - LAG_RELAY)
         relay_done(i - LAG_RELAY - 2)
-        gather_mate(ag - 2)
-
-        @when_group(i)
-        def _():
-            @pl.when(first)
-            def _():
-                load_x(i).wait()
-
-                @pl.when(i + 1 < groups)
-                def _():
-                    load_x(i + 1).start()
-
-            layer_norm(i)
-
-        reduce_pair(i - 1, 1)
-
-        @when_group(i)
-        def _():
-            @pl.when(i == 0)
-            def _():
-                load_up.wait()
-
-            matmul_up()
-
-        reduce_ring(i - 1)
-        gather_sides(ag - 1)
-
-        @when_group(i)
-        def _():
-            @pl.when(i == 0)
-            def _():
-                load_down.wait()
-
-            matmul_down(i, 0)
-            matmul_down(i, 1)
-
-        reduce_pair(i, 0)
-        reduce_last(i - 1)
-        gather_opposite(ag - 1)
-        gather_own(ag)
-
-    @pl.loop(-2, groups + LAG_FIRST + 5)
+        tail_done(i - 4)
+        actions = {
+            "mate": lambda: gather_mate(ag - 2),
+            "norm": lambda: compute_norm(i),
+            "up0": lambda: compute_up(i, 0),
+            "up1": lambda: compute_up(i, 1),
+            "down0": lambda: compute_down(i, 0),
+            "down1": lambda: compute_down(i, 1),
+            "pair0": lambda: reduce_pair(i, 0),
+            "pair1": lambda: reduce_pair(i, 1),
+            "pair1x": lambda: reduce_pair(i - 1, 1),
+            "ring0": lambda: reduce_ring(i - 1, 0),
+            "ring1": lambda: reduce_ring(i - 1, 1),
+            "last": lambda: reduce_last(i - 1),
+            "own": lambda: (gather_own(ag), tail_own(i - 1)),
+            "sides": lambda: (gather_sides(ag - 1), tail_sides(i - 2)),
+            "opp": lambda: (gather_opposite(ag - 1), tail_opposite(i - 2)),
+        }
+        for name in ORDER:
+            actions[name]()
+
+    @pl.loop(-2, groups + jnp.where(first, LAG_FIRST + 5 - TAIL, LAG_RELAY + 3))
     def _(i):
         step(i)
+
+
+def keep_kernel(src, dst, held, in_sem, out_sem):
+    groups = src.shape[0]
+    reads = [pltpu.make_async_copy(src.at[g], held.at[g], in_sem.at[g]) for g in range(groups)]
+    writes = [pltpu.make_async_copy(held.at[g], dst.at[g], out_sem.at[g]) for g in range(groups)]
+    for copy in reads:
+        copy.start()
+    for g in range(groups):
+        reads[g].wait()
+        writes[g].start()
+    for copy in writes:
+        copy.wait()
 
 
 def solution(mesh):
@@ -373,12 +483,22 @@
                 dma((SLOTS, 2)), dma((SLOTS, 2)), dma((SLOTS, 2)), dma((SLOTS, 2)),
                 dma((4, 2)), dma((4, 4)), dma((4, 2)), dma((4, 3)), dma((4, 3)),
                 dma((2, 2)), dma((2, 2)), dma((2, 2)), dma((2, 2)), dma((2,)), dma((2,)), dma((2,)),
+                dma((TAIL, 4)), dma((TAIL, 2)), dma((TAIL, 2)), dma((TAIL, 3)), dma((TAIL, 3)),
             ],
             compiler_params=pltpu.CompilerParams(
                 collective_id=0, has_side_effects=True, vmem_limit_bytes=66_000_000
             ),
             name="mlp_pipeline",
         )(x_blocks, gain_local, up_local, down_local)
-        return out.reshape(1, micro, tokens, width)
+        kept = pl.pallas_call(
+            keep_kernel,
+            out_shape=jax.ShapeDtypeStruct(x_blocks.shape, BF16),
+            in_specs=[pl.BlockSpec(memory_space=pl.ANY)],
+            out_specs=pl.BlockSpec(memory_space=pl.ANY),
+            scratch_shapes=[pltpu.VMEM(x_blocks.shape, BF16), dma((groups,)), dma((groups,))],
+            compiler_params=pltpu.CompilerParams(vmem_limit_bytes=40_000_000),
+            name="keep_result",
+        )(out)
+        return kept.reshape(1, micro, tokens, width)
 
     return jax.shard_map(per_device, mesh=mesh, in_specs=(P("data"), P("stage"), P("stage", None, "tp"), P("stage", "tp", None)), out_specs=P("stage", "data"), check_vma=False)

time: 317 us -> 296 us (0.934)
  local copies, waits for them, and re-layouts: 14.1 us -> 0 us
  Pallas kernels: 302 us -> 295 us
    pallas_call x1, Pallas kernels: 302 us -> 284 us  [per_device(): pl.pallas_call(functools.partial(mlp_kernel, n_stage, n_tp), out_shape=ja...]
    unnamed x1 -> x0, local copies, waits for them, and re-layouts: 14.1 us -> none
    pallas_call x0 -> x1, Pallas kernels: none -> 12 us  [per_device(): pl.pallas_call(keep_kernel, out_shape=jax.ShapeDtypeStruct(x_blocks.shape...]
where the time goes in v2:
time: 296 us; the launch traced here: 295 us
  Pallas kernels  295 us (100%)
    pallas_call x1, Pallas kernels, per_device(): pl.pallas_call(functools.partial(mlp_kernel, n_stage, n_tp), out_shape=ja...  284 us
    pallas_call x1, Pallas kernels, per_device(): pl.pallas_call(keep_kernel, out_shape=jax.ShapeDtypeStruct(x_blocks.shape...  12 us

profile of v2, /device:TPU:121, one launch (start us, length us, event | category | flops | bytes accessed | tf_op | source)
XLA Modules:
  0.0 295.5 jit_solution(6440127779427255911)
XLA Ops:
  0.0 283.5 %mlp_pipeline.1.src = bf16[16,8,16,4096]{3,2,1,0:T(8,128)(2,1)} custom-call(bf16[16,8,16,4096]{3,2,1,0:T(8,128)(2,1)} %bitcast.2, bf16[1,4096]{1,0:T(2,128)(2,1)} %gain_ref.1, bf16[1,4096,1792]{2,1,0:T(8,128)(2,1)} %up_hbm.1, bf16[1,1792,4096]{2,1,0:T(8,128)(2,1)} %down_hbm.1), custom_call_target="tpu_custom_call" | custom-call | tf_op jit(solution)/shard_map/mlp_pipeline/pallas_call | solution.py:456
  283.5 12.0 %keep_result.1 = bf16[16,8,16,4096]{3,2,1,0:T(8,128)(2,1)} custom-call(bf16[16,8,16,4096]{3,2,1,0:T(8,128)(2,1)} %mlp_pipeline.1.src), custom_call_target="tpu_custom_call" | custom-call | tf_op jit(solution)/shard_map/keep_result/pallas_call | solution.py:493

commit v3 on v2

--- a/solution.py
+++ b/solution.py
@@ -18,7 +18,7 @@
 LAG_RELAY = 6
 LN_ROWS = 64
 UP_PIECES = 1
-ORDER = ("mate", "norm", "up0", "ring0", "ring1", "down0", "sides", "down1", "last", "pair0", "pair1", "own", "opp")
+ORDER = ("mate", "own", "norm", "up0", "ring0", "ring1", "down0", "sides", "rest", "down1", "pair0", "last", "pair1", "opp")
 F32, BF16 = jnp.float32, jnp.bfloat16
 
 
@@ -90,8 +90,9 @@
     def in_slot(g):
         return jnp.where(first, groups + lax.rem(g, STAGING), g)
 
-    def side_copy(g, way):
-        return remote(acts.at[g, rank], acts.at[g, rank], side_s.at[lax.rem(g, 4), way], side_r.at[g, way], (right, left)[way])
+    def side_copy(g, way, h):
+        ref = acts.at[g, rank, :, cols[h]]
+        return remote(ref, ref, side_s.at[lax.rem(g, 4), way, h], side_r.at[g, way, h], (right, left)[way])
 
     def fwd_copy(g, way):
         block = (block_l, block_r)[way]
@@ -114,8 +115,10 @@
         @when_gathered(g)
         def _():
             next_copy(g).wait_recv()
-            side_copy(g, 0).start()
-            side_copy(g, 1).start()
+            side_copy(g, 0, 0).start()
+            side_copy(g, 1, 1).start()
+            side_copy(g, 0, 1).start()
+            side_copy(g, 1, 0).start()
 
             @pl.when(jnp.logical_not(first))
             def _():
@@ -124,10 +127,15 @@
     def gather_sides(g):
         @when_gathered(g)
         def _():
-            side_copy(g, 0).wait_recv()
-            side_copy(g, 1).wait_recv()
-            fwd_copy(g, 0).start()
-            fwd_copy(g, 1).start()
+            for way in range(2):
+                side_copy(g, way, way).wait_recv()
+                fwd_copy(g, way).start()
+
+    def gather_rest(g):
+        @when_gathered(g)
+        def _():
+            for way in range(2):
+                side_copy(g, way, 1 - way).wait_recv()
 
             @pl.when(jnp.logical_not(first))
             def _():
@@ -159,7 +167,8 @@
         @when_gathered(g)
         def _():
             for way in range(2):
-                side_copy(g, way).wait_send()
+                side_copy(g, way, 0).wait_send()
+                side_copy(g, way, 1).wait_send()
                 fwd_copy(g, way).wait_send()
             for which in range(3):
                 back_copy(g, which).wait_send()
@@ -406,17 +415,16 @@
             "mate": lambda: gather_mate(ag - 2),
             "norm": lambda: compute_norm(i),
             "up0": lambda: compute_up(i, 0),
-            "up1": lambda: compute_up(i, 1),
             "down0": lambda: compute_down(i, 0),
             "down1": lambda: compute_down(i, 1),
             "pair0": lambda: reduce_pair(i, 0),
             "pair1": lambda: reduce_pair(i, 1),
-            "pair1x": lambda: reduce_pair(i - 1, 1),
             "ring0": lambda: reduce_ring(i - 1, 0),
             "ring1": lambda: reduce_ring(i - 1, 1),
             "last": lambda: reduce_last(i - 1),
-            "own": lambda: (gather_own(ag), tail_own(i - 1)),
+            "own": lambda: (gather_own(ag - 1), tail_own(i - 2)),
             "sides": lambda: (gather_sides(ag - 1), tail_sides(i - 2)),
+            "rest": lambda: gather_rest(ag - 1),
             "opp": lambda: (gather_opposite(ag - 1), tail_opposite(i - 2)),
         }
         for name in ORDER:
@@ -478,10 +486,10 @@
                 pltpu.VMEM((2, 2, rows, half), BF16),
                 pltpu.VMEM((2, rows, width), BF16),
                 dma((2,)), dma((STAGING,)),
-                dma((groups,)), dma((groups, 2)), dma((groups, 2)), dma((groups, 4)),
+                dma((groups,)), dma((groups, 2, 2)), dma((groups, 2)), dma((groups, 4)),
                 dma((groups, 3)), dma((groups, 3)), dma((groups,)),
                 dma((SLOTS, 2)), dma((SLOTS, 2)), dma((SLOTS, 2)), dma((SLOTS, 2)),
-                dma((4, 2)), dma((4, 4)), dma((4, 2)), dma((4, 3)), dma((4, 3)),
+                dma((4, 2, 2)), dma((4, 4)), dma((4, 2)), dma((4, 3)), dma((4, 3)),
                 dma((2, 2)), dma((2, 2)), dma((2, 2)), dma((2, 2)), dma((2,)), dma((2,)), dma((2,)),
                 dma((TAIL, 4)), dma((TAIL, 2)), dma((TAIL, 2)), dma((TAIL, 3)), dma((TAIL, 3)),
             ],

time: 296 us -> 284 us (0.959)
  Pallas kernels: 295 us -> 284 us
    pallas_call x1, Pallas kernels: 284 us -> 272 us  [per_device(): pl.pallas_call(functools.partial(mlp_kernel, n_stage, n_tp), out_shape=ja...]
where the time goes in v3:
time: 284 us
  Pallas kernels  284 us (100%)
    pallas_call x1, Pallas kernels, per_device(): pl.pallas_call(functools.partial(mlp_kernel, n_stage, n_tp), out_shape=ja...  272 us
    pallas_call x1, Pallas kernels, per_device(): pl.pallas_call(keep_kernel, out_shape=jax.ShapeDtypeStruct(x_blocks.shape...  12 us

profile of v3, /device:TPU:121, one launch (start us, length us, event | category | flops | bytes accessed | tf_op | source)
XLA Modules:
  0.0 283.7 jit_solution(13986844599517480522)
XLA Ops:
  0.0 271.7 %mlp_pipeline.1.src = bf16[16,8,16,4096]{3,2,1,0:T(8,128)(2,1)} custom-call(bf16[16,8,16,4096]{3,2,1,0:T(8,128)(2,1)} %bitcast.2, bf16[1,4096]{1,0:T(2,128)(2,1)} %gain_ref.1, bf16[1,4096,1792]{2,1,0:T(8,128)(2,1)} %up_hbm.1, bf16[1,1792,4096]{2,1,0:T(8,128)(2,1)} %down_hbm.1), custom_call_target="tpu_custom_call" | custom-call | tf_op jit(solution)/shard_map/mlp_pipeline/pallas_call | solution.py:464
  271.7 12.0 %keep_result.1 = bf16[16,8,16,4096]{3,2,1,0:T(8,128)(2,1)} custom-call(bf16[16,8,16,4096]{3,2,1,0:T(8,128)(2,1)} %mlp_pipeline.1.src), custom_call_target="tpu_custom_call" | custom-call | tf_op jit(solution)/shard_map/keep_result/pallas_call | solution.py:501

commit v4 on v3

--- a/solution.py
+++ b/solution.py
@@ -15,10 +15,10 @@
 STAGING = 3
 LAG_FIRST = 13
 TAIL = 2
-LAG_RELAY = 6
+LAG_RELAY = 5
 LN_ROWS = 64
 UP_PIECES = 1
-ORDER = ("mate", "own", "norm", "up0", "ring0", "ring1", "down0", "sides", "rest", "down1", "pair0", "last", "pair1", "opp")
+ORDER = ("mate", "own", "norm", "up0", "ring0", "ring1", "down0", "sides", "down1", "pair0", "rest", "last", "pair1", "opp")
 F32, BF16 = jnp.float32, jnp.bfloat16
 
 
@@ -92,24 +92,24 @@
 
     def side_copy(g, way, h):
         ref = acts.at[g, rank, :, cols[h]]
-        return remote(ref, ref, side_s.at[lax.rem(g, 4), way, h], side_r.at[g, way, h], (right, left)[way])
+        return remote(ref, ref, side_s.at[lax.rem(g, 4), way, h], side_r.at[lax.rem(g, 4), way, h], (right, left)[way])
 
     def fwd_copy(g, way):
         block = (block_l, block_r)[way]
         ref = acts.at[g, block, :, cols[way]]
-        return remote(ref, ref, fwd_s.at[lax.rem(g, 4), way], opp_r.at[g, way], (right, left)[way])
+        return remote(ref, ref, fwd_s.at[lax.rem(g, 4), way], opp_r.at[lax.rem(g, 4), way], (right, left)[way])
 
     def mate_copy(g, which):
         block = (rank, block_l, block_r, block_o)[which]
-        return remote(acts.at[g, block], acts.at[g, block], mate_s.at[lax.rem(g, 4), which], mate_r.at[g, which], mate)
+        return remote(acts.at[g, block], acts.at[g, block], mate_s.at[lax.rem(g, 4), which], mate_r.at[lax.rem(g, 4), which], mate)
 
     def back_copy(g, which):
         block = (block_l, block_r, block_o)[which]
-        return remote(acts.at[g, block], y_hbm.at[g, block], back_s.at[lax.rem(g, 4), which], back_r.at[g, which], behind)
+        return remote(acts.at[g, block], y_hbm.at[g, block], back_s.at[lax.rem(g, 4), which], back_r.at[lax.rem(g, 4), which], behind)
 
     def next_copy(g):
         slot = lax.rem(g, 2)
-        return remote(shard.at[slot], acts.at[g, rank], next_s.at[slot], own_r.at[g], ahead)
+        return remote(shard.at[slot], acts.at[g, rank], next_s.at[slot], own_r.at[lax.rem(g, 4)], ahead)
 
     def gather_own(g):
         @when_gathered(g)
@@ -235,7 +235,7 @@
 
     def tail_mate_copy(g, which):
         index, block = g - (groups - TAIL), (block_l, block_r, block_o)[which]
-        return remote(acts.at[g + TAIL, block], y_hbm.at[g, block], tail_mate_s.at[index, which], relay_r.at[g, which], mate)
+        return remote(acts.at[g + TAIL, block], y_hbm.at[g, block], tail_mate_s.at[index, which], relay_r.at[lax.rem(g, 8), which], mate)
 
     def tail_own(g):
         @when_tail(g)
@@ -261,6 +261,20 @@
             tail_mate_copy(g, 2).start()
             tail_keep_copy(g, 2).start()
 
+    def tail_start(i):
+        @pl.when(i == groups)
+        def _():
+            tail_own(i - 2)
+
+    def tail_finish(i):
+        @pl.when(i == groups)
+        def _():
+            tail_own(i - 1)
+            for back in (2, 1):
+                tail_sides(i - back)
+            for back in (2, 1):
+                tail_opposite(i - back)
+
     def tail_done(g):
         @when_tail(g)
         def _():
@@ -276,7 +290,7 @@
 
     def out_copy(g):
         slot = lax.rem(g, 2)
-        return remote(shard.at[slot], y_hbm.at[g, rank], out_s.at[slot], out_r.at[g], mate)
+        return remote(shard.at[slot], y_hbm.at[g, rank], out_s.at[slot], out_r.at[lax.rem(g, 8)], mate)
 
     def reduce_last(g):
         @when_group(g)
@@ -325,7 +339,7 @@
     def relay_copy(g, which):
         block = (block_l, block_r, block_o)[which]
         ref = y_hbm.at[g, block]
-        return remote(ref, ref, relay_s.at[lax.rem(g, 4), which], relay_r.at[g, which], mate)
+        return remote(ref, ref, relay_s.at[lax.rem(g, 4), which], relay_r.at[lax.rem(g, 8), which], mate)
 
     def relay(g):
         @pl.when((g >= 0) & (g < groups) & jnp.logical_not(is_tail(g)))
@@ -420,12 +434,12 @@
             "pair0": lambda: reduce_pair(i, 0),
             "pair1": lambda: reduce_pair(i, 1),
             "ring0": lambda: reduce_ring(i - 1, 0),
-            "ring1": lambda: reduce_ring(i - 1, 1),
-            "last": lambda: reduce_last(i - 1),
-            "own": lambda: (gather_own(ag - 1), tail_own(i - 2)),
-            "sides": lambda: (gather_sides(ag - 1), tail_sides(i - 2)),
+            "ring1": lambda: (reduce_ring(i - 1, 1), tail_start(i)),
+            "last": lambda: (reduce_last(i - 1), tail_finish(i)),
+            "own": lambda: gather_own(ag - 1),
+            "sides": lambda: gather_sides(ag - 1),
             "rest": lambda: gather_rest(ag - 1),
-            "opp": lambda: (gather_opposite(ag - 1), tail_opposite(i - 2)),
+            "opp": lambda: gather_opposite(ag - 1),
         }
         for name in ORDER:
             actions[name]()
@@ -486,8 +500,8 @@
                 pltpu.VMEM((2, 2, rows, half), BF16),
                 pltpu.VMEM((2, rows, width), BF16),
                 dma((2,)), dma((STAGING,)),
-                dma((groups,)), dma((groups, 2, 2)), dma((groups, 2)), dma((groups, 4)),
-                dma((groups, 3)), dma((groups, 3)), dma((groups,)),
+                dma((4,)), dma((4, 2, 2)), dma((4, 2)), dma((4, 4)),
+                dma((4, 3)), dma((8, 3)), dma((8,)),
                 dma((SLOTS, 2)), dma((SLOTS, 2)), dma((SLOTS, 2)), dma((SLOTS, 2)),
                 dma((4, 2, 2)), dma((4, 4)), dma((4, 2)), dma((4, 3)), dma((4, 3)),
                 dma((2, 2)), dma((2, 2)), dma((2, 2)), dma((2, 2)), dma((2,)), dma((2,)), dma((2,)),

time: 284 us -> 280 us (0.986)
  Pallas kernels: 284 us -> 280 us
    pallas_call x1, Pallas kernels: 272 us -> 268 us  [per_device(): pl.pallas_call(functools.partial(mlp_kernel, n_stage, n_tp), out_shape=ja...]
where the time goes in v4:
time: 280 us
  Pallas kernels  280 us (100%)
    pallas_call x1, Pallas kernels, per_device(): pl.pallas_call(functools.partial(mlp_kernel, n_stage, n_tp), out_shape=ja...  268 us
    pallas_call x1, Pallas kernels, per_device(): pl.pallas_call(keep_kernel, out_shape=jax.ShapeDtypeStruct(x_blocks.shape...  12 us

profile of v4, /device:TPU:121, one launch (start us, length us, event | category | flops | bytes accessed | tf_op | source)
XLA Modules:
  0.0 279.6 jit_solution(17189352937381235485)
XLA Ops:
  0.0 267.6 %mlp_pipeline.1.src = bf16[16,8,16,4096]{3,2,1,0:T(8,128)(2,1)} custom-call(bf16[16,8,16,4096]{3,2,1,0:T(8,128)(2,1)} %bitcast.2, bf16[1,4096]{1,0:T(2,128)(2,1)} %gain_ref.1, bf16[1,4096,1792]{2,1,0:T(8,128)(2,1)} %up_hbm.1, bf16[1,1792,4096]{2,1,0:T(8,128)(2,1)} %down_hbm.1), custom_call_target="tpu_custom_call" | custom-call | tf_op jit(solution)/shard_map/mlp_pipeline/pallas_call | solution.py:478
  267.7 12.0 %keep_result.1 = bf16[16,8,16,4096]{3,2,1,0:T(8,128)(2,1)} custom-call(bf16[16,8,16,4096]{3,2,1,0:T(8,128)(2,1)} %mlp_pipeline.1.src), custom_call_target="tpu_custom_call" | custom-call | tf_op jit(solution)/shard_map/keep_result/pallas_call | solution.py:515
